TPU v7x, 32 devices: a whole 2x2x4 slice. The times are simulated.
32 devices in a mesh: batch: 2 (over x), row: 4 (over z), col: 4 (over y, core).
Axes of the slice: x: 2, y: 2, z: 4, core: 2. Of those that a mesh axis runs over, the one named last changes fastest.
Arguments:
- spd_blocks: float32 [96, 128, 6144], P(('batch', 'row'), None, 'col'), parts along dimension 0
Outputs:
- output: float32 [96, 128, 6144], P(('batch', 'row'), None, 'col'), parts along dimension 0
There are 2 independent parts. A program takes and returns all parts, laid end to end along the dimension named above; each array names one.
All inputs are finite; a program needn't handle non-finite values.
Results may differ from a plain program's by a relative error of at most 0.001.
Values are sent between devices in bfloat16 or wider.
A program may use at most 1 GiB of HBM per device.

v0:
```python
import functools
import jax
import jax.numpy as jnp
from jax import lax
from jax.sharding import PartitionSpec as P, NamedSharding


def transposed_panel(row_panel, row_id, col_id, row_devs, col_devs, row_skip, col_skip):
    row_blocks = row_panel.shape[0]
    blk_size = row_panel.shape[1]
    if row_devs >= col_devs:
        grid_ratio = row_devs // col_devs
        blk_shift = (row_skip * row_devs - col_skip * col_devs) // col_devs
        pick_mask = (jnp.arange(grid_ratio) == row_id // col_devs) & (row_id % col_devs == col_id)
        spread = (row_panel[:, None] * pick_mask.astype(jnp.bfloat16)[None, :, None, None]).reshape(row_blocks * grid_ratio, blk_size, blk_size)
        if blk_shift >= 0:
            spread = jnp.pad(spread, ((blk_shift, 0), (0, 0), (0, 0)))
        else:
            spread = spread[-blk_shift:]
    else:
        grid_ratio = col_devs // row_devs
        blk_shift = (col_skip * col_devs - row_skip * row_devs) // row_devs
        if blk_shift >= 0:
            shifted = row_panel[blk_shift:]
        else:
            shifted = jnp.pad(row_panel, ((-blk_shift, 0), (0, 0), (0, 0)))
        grouped = shifted.reshape(shifted.shape[0] // grid_ratio, grid_ratio, blk_size, blk_size)
        chosen = lax.dynamic_index_in_dim(grouped, col_id // row_devs, axis=1, keepdims=False)
        spread = jnp.where(row_id == col_id % row_devs, chosen, jnp.zeros_like(chosen))
    return lax.psum(spread, "row")


def solution(mesh):
    row_devs = mesh.shape["row"]
    col_devs = mesh.shape["col"]

    def factor_local(a_loc):
        row_blocks, blk_size, local_cols = a_loc.shape
        col_blocks = local_cols // blk_size
        blk_count = row_blocks * row_devs
        row_id = lax.axis_index("row")
        col_id = lax.axis_index("col")
        eye_blk = jnp.eye(blk_size, dtype=jnp.float32)

        def panel_step(step_idx, window):
            win_rows, win_cols = window.shape
            win_rblk = win_rows // blk_size
            row_skip = row_blocks - win_rblk
            col_skip = col_blocks - win_cols // blk_size
            own_col = col_id == step_idx % col_devs
            is_owner = own_col & (row_id == step_idx % row_devs)
            col_off = (step_idx // col_devs - col_skip) * blk_size
            col_blk = lax.dynamic_slice_in_dim(window, col_off, blk_size, axis=1)
            diag_blk = lax.dynamic_slice_in_dim(col_blk, (step_idx // row_devs - row_skip) * blk_size, blk_size, axis=0)
            diag_own = jnp.tril(jnp.linalg.cholesky(jnp.where(is_owner, diag_blk, eye_blk)))
            diag_fac = lax.psum(jnp.where(is_owner, diag_own, 0.0), "row")
            diag_fac = jnp.where(own_col, diag_fac, eye_blk)
            solved = lax.linalg.triangular_solve(diag_fac, col_blk, left_side=False, lower=True, transpose_a=True)
            row_ids = (row_skip + jnp.arange(win_rblk)) * row_devs + row_id
            below_mask = (row_ids > step_idx)[:, None, None]
            on_diag = (row_ids == step_idx)[:, None, None]
            solved_blocks = solved.reshape(win_rblk, blk_size, blk_size)
            prior_col = col_blk.reshape(win_rblk, blk_size, blk_size)
            new_col = jnp.where(below_mask, solved_blocks, jnp.where(on_diag, diag_fac[None], prior_col))
            new_col = jnp.where(own_col, new_col, prior_col).reshape(win_rows, blk_size)
            window = lax.dynamic_update_slice_in_dim(window, new_col, col_off, axis=1)
            row_panel = lax.psum(jnp.where(below_mask & own_col, solved_blocks, 0.0).astype(jnp.bfloat16), "col")
            col_panel = transposed_panel(row_panel, row_id, col_id, row_devs, col_devs, row_skip, col_skip)
            update = lax.dot_general(row_panel.reshape(win_rows, blk_size), col_panel.reshape(win_cols, blk_size), (((1,), (1,)), ((), ())), preferred_element_type=jnp.float32)
            return window - update

        work_mat = a_loc.reshape(row_blocks * blk_size, local_cols)
        phase_count = min(blk_count, 8)
        bounds = [(phase_idx * blk_count) // phase_count for phase_idx in range(phase_count + 1)]
        for phase_idx in range(phase_count):
            row_start = (bounds[phase_idx] // row_devs) * blk_size
            col_start = (bounds[phase_idx] // col_devs) * blk_size
            window = lax.fori_loop(bounds[phase_idx], bounds[phase_idx + 1], panel_step, work_mat[row_start:, col_start:])
            work_mat = lax.dynamic_update_slice(work_mat, window, (row_start, col_start))
        row_blk_ids = jnp.arange(row_blocks) * row_devs + row_id
        col_blk_ids = jnp.arange(col_blocks) * col_devs + col_id
        keep_mask = row_blk_ids[:, None, None, None] >= col_blk_ids[None, None, :, None]
        factor = jnp.where(keep_mask, work_mat.reshape(row_blocks, blk_size, col_blocks, blk_size), 0.0)
        return factor.reshape(row_blocks, blk_size, local_cols)

    blk_spec = P(("batch", "row"), None, "col")
    return jax.shard_map(factor_local, mesh=mesh, in_specs=(blk_spec,), out_specs=blk_spec, check_vma=False)
```

profile of v0, /device:TPU:31, one launch (start us, length us, event | category | flops | bytes accessed | tf_op | source)
XLA Modules:
  0.0 6546.5 jit_solution(10407261180541380101)
XLA Ops:
  14.8 854.9 %while.152 = (s32[]{:T(128)}, f32[1536,1536]{1,0:T(8,128)}, s32[]{:T(128)}, s32[]{:T(128)}, pred[1]{0:T(512)(128)(4,1)}, /*index=5*/s32[]{:T(128)}, s32[]{:T(128...) while((s32[]{:T(128)}, f32[1536,1536]{1,0:T(8,128)}, ...), condition=%wide.region_6.8_spmd.clone.clone, body=%wide.region_0.7_spmd.clone.clone.sunk | while | flops 910262464 | bytes 32572976 | solution.py:78
  111.2 35.3 all-reduce.29.cloned.1.call-done
  254.0 35.2 all-reduce.29.cloned.1.call-done
  360.1 34.6 all-reduce.27.cloned.1.call-done
  397.4 35.3 all-reduce.29.cloned.1.call-done
  540.2 35.2 all-reduce.29.cloned.1.call-done
  682.8 35.2 all-reduce.29.cloned.1.call-done
  825.4 35.2 all-reduce.29.cloned.1.call-done
  876.5 845.7 %while.153 = (s32[]{:T(128)}, f32[1408,1408]{1,0:T(8,128)}, s32[]{:T(128)}, s32[]{:T(128)}, pred[1]{0:T(512)(128)(4,1)}, /*index=5*/s32[]{:T(128)}, s32[]{:T(128...) while((s32[]{:T(128)}, f32[1408,1408]{1,0:T(8,128)}, ...), condition=%wide.region_11.13_spmd.clone.clone, body=%wide.region_7.12_spmd.clone.clone.sunk | while | flops 788119808 | bytes 28542608 | solution.py:78
  938.8 34.4 all-reduce.33.cloned.1.call-done
  976.0 35.0 all-reduce.35.cloned.1.call-done
  1116.7 34.9 all-reduce.35.cloned.1.call-done
  1257.2 34.9 all-reduce.35.cloned.1.call-done
  1397.7 34.9 all-reduce.35.cloned.1.call-done
  1501.9 34.4 all-reduce.33.cloned.1.call-done
  1539.1 34.9 all-reduce.35.cloned.1.call-done
  1679.6 34.9 all-reduce.35.cloned.1.call-done
  1734.4 827.3 %while.154 = (s32[]{:T(128)}, f32[1152,1152]{1,0:T(8,128)}, s32[]{:T(128)}, s32[]{:T(128)}, pred[1]{0:T(512)(128)(4,1)}, /*index=5*/s32[]{:T(128)}, s32[]{:T(128...) while((s32[]{:T(128)}, f32[1152,1152]{1,0:T(8,128)}, ...), condition=%wide.region_16.18_spmd.clone.clone, body=%wide.region_12.17_spmd.clone.clone.sunk | while | flops 569098432 | bytes 21268108 | solution.py:78
  1832.3 34.0 all-reduce.41.cloned.1.call-done
  1969.9 34.2 all-reduce.41.cloned.1.call-done
  2071.7 34.2 all-reduce.39.cloned.1.call-done
  2108.6 34.0 all-reduce.41.cloned.1.call-done
  2246.2 34.0 all-reduce.41.cloned.1.call-done
  2383.8 34.1 all-reduce.41.cloned.1.call-done
  2521.4 34.4 all-reduce.41.cloned.1.call-done
  2571.7 818.3 %while.155 = (s32[]{:T(128)}, f32[1024,1024]{1,0:T(8,128)}, s32[]{:T(128)}, s32[]{:T(128)}, pred[1]{0:T(512)(128)(4,1)}, /*index=5*/s32[]{:T(128)}, s32[]{:T(128...) while((s32[]{:T(128)}, f32[1024,1024]{1,0:T(8,128)}, ...), condition=%wide.region_21.23_spmd.clone.clone, body=%wide.region_17.22_spmd.clone.clone.sunk | while | flops 472219840 | bytes 18024072 | solution.py:78
  2633.5 34.1 all-reduce.45.cloned.1.call-done
  2670.2 33.8 all-reduce.47.cloned.1.call-done
  2806.3 33.8 all-reduce.47.cloned.1.call-done
  3178.4 34.1 all-reduce.45.cloned.1.call-done
  3215.1 33.9 all-reduce.47.cloned.1.call-done
  3396.5 781.1 %while.156 = (s32[]{:T(128)}, f32[768,768]{1,0:T(8,128)S(1)}, s32[]{:T(128)}, s32[]{:T(128)}, pred[1]{0:T(512)(128)(4,1)}, /*index=5*/s32[]{:T(128)}, s32[]{:T(1...) while((s32[]{:T(128)}, f32[768,768]{1,0:T(8,128)S(1)}, ...), condition=%wide.region_26.28_spmd.clone.clone, body=%wide.region_22.27_spmd.clone.clone.sunk | while | flops 303726784 | bytes 12322428 | solution.py:78
  3411.1 34.2 all-reduce.49.cloned.1.call-done
  3491.1 34.1 all-reduce.53.cloned.1.call-done
  3541.1 34.2 all-reduce.49.cloned.1.call-done
  3621.2 34.1 all-reduce.53.cloned.1.call-done
  3671.2 34.2 all-reduce.49.cloned.1.call-done
  3716.5 33.9 all-reduce.51.cloned.1.call-done
  3752.1 34.1 all-reduce.53.cloned.1.call-done
  3802.1 34.2 all-reduce.49.cloned.1.call-done
  3882.2 34.0 all-reduce.53.cloned.1.call-done
  3932.0 34.2 all-reduce.49.cloned.1.call-done
  4012.1 34.0 all-reduce.53.cloned.1.call-done
  4061.9 34.2 all-reduce.49.cloned.1.call-done
  4142.0 34.1 all-reduce.53.cloned.1.call-done
  4180.5 800.2 %while.157 = (s32[]{:T(128)}, f32[640,640]{1,0:T(8,128)}, s32[]{:T(128)}, s32[]{:T(128)}, pred[1]{0:T(512)(128)(4,1)}, /*index=5*/s32[]{:T(128)}, s32[]{:T(128)}...) while((s32[]{:T(128)}, f32[640,640]{1,0:T(8,128)}, ...), condition=%wide.region_31.33_spmd.clone.clone, body=%wide.region_27.32_spmd.clone.clone.sunk | while | flops 232112320 | bytes 9864822 | solution.py:78
  4984.5 773.3 %while.158 = (s32[]{:T(128)}, f32[384,384]{1,0:T(8,128)S(1)}, s32[]{:T(128)}, s32[]{:T(128)}, pred[1]{0:T(512)(128)(4,1)}, /*index=5*/s32[]{:T(128)}, s32[]{:T(1...) while((s32[]{:T(128)}, f32[384,384]{1,0:T(8,128)S(1)}, ...), condition=%wide.region_36.38_spmd.clone.clone, body=%wide.region_32.37_spmd.clone.clone.sunk | while | flops 114147504 | bytes 5736042 | solution.py:78
  4999.0 34.2 all-reduce.61.cloned.1.call-done
  5127.8 34.1 all-reduce.61.cloned.1.call-done
  5207.1 33.8 all-reduce.65.cloned.1.call-done
  5256.5 34.1 all-reduce.61.cloned.1.call-done
  5385.9 34.1 all-reduce.61.cloned.1.call-done
  5465.3 33.8 all-reduce.65.cloned.1.call-done
  5514.7 34.1 all-reduce.61.cloned.1.call-done
  5643.4 34.1 all-reduce.61.cloned.1.call-done
  5758.7 771.1 %while.159 = (s32[]{:T(128)}, f32[256,256]{1,0:T(8,128)S(1)}, s32[]{:T(128)}, s32[]{:T(128)}, pred[1]{0:T(512)(128)(4,1)}, /*index=5*/s32[]{:T(128)}, s32[]{:T(1...) while((s32[]{:T(128)}, f32[256,256]{1,0:T(8,128)S(1)}, ...), condition=%wide.region_41.43_spmd.clone.clone, body=%wide.region_37.42_spmd.clone.clone.sunk | while | flops 67797160 | bytes 4064860 | solution.py:78
  5773.2 34.1 all-reduce.67.cloned.1.call-done
  5853.1 33.9 all-reduce.71.cloned.1.call-done
  5902.4 34.1 all-reduce.67.cloned.1.call-done
  6030.6 34.1 all-reduce.67.cloned.1.call-done
  6158.7 34.1 all-reduce.67.cloned.1.call-done
  6237.7 33.9 all-reduce.71.cloned.1.call-done
  6286.9 34.1 all-reduce.67.cloned.1.call-done
  6415.9 34.1 all-reduce.67.cloned.1.call-done
  (1213 shorter events, 4603.1 us)
Async XLA Ops:
  30.7 77.8 %all-reduce.27.cloned.1.call-start = ((), (), s32[]{:S(2)}) async-start(), calls=%async_computation.1 | async-start | bytes 786432 | tf_op jit(solution)/shard_map/while/body/eval_jaxpr/psum | solution.py:67
  74.6 71.9 %all-reduce.29.cloned.1.call-start = ((), (), s32[]{:S(2)}) async-start(), calls=%async_computation.2 | async-start | bytes 786432 | tf_op jit(solution)/shard_map/while/body/eval_jaxpr/psum | solution.py:30
  171.5 79.7 %all-reduce.27.cloned.1.call-start = ((), (), s32[]{:S(2)}) async-start(), calls=%async_computation.1 | async-start | bytes 786432 | tf_op jit(solution)/shard_map/while/body/eval_jaxpr/psum | solution.py:67
  217.4 71.8 %all-reduce.29.cloned.1.call-start = ((), (), s32[]{:S(2)}) async-start(), calls=%async_computation.2 | async-start | bytes 786432 | tf_op jit(solution)/shard_map/while/body/eval_jaxpr/psum | solution.py:30
  314.2 80.5 %all-reduce.27.cloned.1.call-start = ((), (), s32[]{:S(2)}) async-start(), calls=%async_computation.1 | async-start | bytes 786432 | tf_op jit(solution)/shard_map/while/body/eval_jaxpr/psum | solution.py:67
  360.0 72.7 %all-reduce.29.cloned.1.call-start = ((), (), s32[]{:S(2)}) async-start(), calls=%async_computation.2 | async-start | bytes 786432 | tf_op jit(solution)/shard_map/while/body/eval_jaxpr/psum | solution.py:30
  457.7 79.7 %all-reduce.27.cloned.1.call-start = ((), (), s32[]{:S(2)}) async-start(), calls=%async_computation.1 | async-start | bytes 786432 | tf_op jit(solution)/shard_map/while/body/eval_jaxpr/psum | solution.py:67
  504.4 70.9 %all-reduce.29.cloned.1.call-start = ((), (), s32[]{:S(2)}) async-start(), calls=%async_computation.2 | async-start | bytes 786432 | tf_op jit(solution)/shard_map/while/body/eval_jaxpr/psum | solution.py:30
  600.4 79.7 %all-reduce.27.cloned.1.call-start = ((), (), s32[]{:S(2)}) async-start(), calls=%async_computation.1 | async-start | bytes 786432 | tf_op jit(solution)/shard_map/while/body/eval_jaxpr/psum | solution.py:67
  646.2 71.8 %all-reduce.29.cloned.1.call-start = ((), (), s32[]{:S(2)}) async-start(), calls=%async_computation.2 | async-start | bytes 786432 | tf_op jit(solution)/shard_map/while/body/eval_jaxpr/psum | solution.py:30
  743.0 79.7 %all-reduce.27.cloned.1.call-start = ((), (), s32[]{:S(2)}) async-start(), calls=%async_computation.1 | async-start | bytes 786432 | tf_op jit(solution)/shard_map/while/body/eval_jaxpr/psum | solution.py:67
  788.8 71.8 %all-reduce.29.cloned.1.call-start = ((), (), s32[]{:S(2)}) async-start(), calls=%async_computation.2 | async-start | bytes 786432 | tf_op jit(solution)/shard_map/while/body/eval_jaxpr/psum | solution.py:30
  892.9 80.3 %all-reduce.33.cloned.1.call-start = ((), (), s32[]{:S(2)}) async-start(), calls=%async_computation.4 | async-start | bytes 720896 | tf_op jit(solution)/shard_map/while/body/eval_jaxpr/psum | solution.py:67
  938.8 72.2 %all-reduce.35.cloned.1.call-start = ((), (), s32[]{:S(2)}) async-start(), calls=%async_computation.5 | async-start | bytes 720896 | tf_op jit(solution)/shard_map/while/body/eval_jaxpr/psum | solution.py:30
  1034.6 79.3 %all-reduce.33.cloned.1.call-start = ((), (), s32[]{:S(2)}) async-start(), calls=%async_computation.4 | async-start | bytes 720896 | tf_op jit(solution)/shard_map/while/body/eval_jaxpr/psum | solution.py:67
  1081.1 70.4 %all-reduce.35.cloned.1.call-start = ((), (), s32[]{:S(2)}) async-start(), calls=%async_computation.5 | async-start | bytes 720896 | tf_op jit(solution)/shard_map/while/body/eval_jaxpr/psum | solution.py:30
  1175.1 79.3 %all-reduce.33.cloned.1.call-start = ((), (), s32[]{:S(2)}) async-start(), calls=%async_computation.4 | async-start | bytes 720896 | tf_op jit(solution)/shard_map/while/body/eval_jaxpr/psum | solution.py:67
  1220.8 71.2 %all-reduce.35.cloned.1.call-start = ((), (), s32[]{:S(2)}) async-start(), calls=%async_computation.5 | async-start | bytes 720896 | tf_op jit(solution)/shard_map/while/body/eval_jaxpr/psum | solution.py:30
  1315.6 79.3 %all-reduce.33.cloned.1.call-start = ((), (), s32[]{:S(2)}) async-start(), calls=%async_computation.4 | async-start | bytes 720896 | tf_op jit(solution)/shard_map/while/body/eval_jaxpr/psum | solution.py:67
  1361.3 71.2 %all-reduce.35.cloned.1.call-start = ((), (), s32[]{:S(2)}) async-start(), calls=%async_computation.5 | async-start | bytes 720896 | tf_op jit(solution)/shard_map/while/body/eval_jaxpr/psum | solution.py:30
  1456.1 80.2 %all-reduce.33.cloned.1.call-start = ((), (), s32[]{:S(2)}) async-start(), calls=%async_computation.4 | async-start | bytes 720896 | tf_op jit(solution)/shard_map/while/body/eval_jaxpr/psum | solution.py:67
  1501.9 72.1 %all-reduce.35.cloned.1.call-start = ((), (), s32[]{:S(2)}) async-start(), calls=%async_computation.5 | async-start | bytes 720896 | tf_op jit(solution)/shard_map/while/body/eval_jaxpr/psum | solution.py:30
  1597.5 79.3 %all-reduce.33.cloned.1.call-start = ((), (), s32[]{:S(2)}) async-start(), calls=%async_computation.4 | async-start | bytes 720896 | tf_op jit(solution)/shard_map/while/body/eval_jaxpr/psum | solution.py:67
  1644.1 70.4 %all-reduce.35.cloned.1.call-start = ((), (), s32[]{:S(2)}) async-start(), calls=%async_computation.5 | async-start | bytes 720896 | tf_op jit(solution)/shard_map/while/body/eval_jaxpr/psum | solution.py:30
  1750.6 79.0 %all-reduce.39.cloned.1.call-start = ((), (), s32[]{:S(2)}) async-start(), calls=%async_computation.7 | async-start | bytes 589824 | tf_op jit(solution)/shard_map/while/body/eval_jaxpr/psum | solution.py:67
  1888.1 79.1 %all-reduce.39.cloned.1.call-start = ((), (), s32[]{:S(2)}) async-start(), calls=%async_computation.7 | async-start | bytes 589824 | tf_op jit(solution)/shard_map/while/body/eval_jaxpr/psum | solution.py:67
  2025.9 79.9 %all-reduce.39.cloned.1.call-start = ((), (), s32[]{:S(2)}) async-start(), calls=%async_computation.7 | async-start | bytes 589824 | tf_op jit(solution)/shard_map/while/body/eval_jaxpr/psum | solution.py:67
  2071.6 71.0 %all-reduce.41.cloned.1.call-start = ((), (), s32[]{:S(2)}) async-start(), calls=%async_computation.8 | async-start | bytes 589824 | tf_op jit(solution)/shard_map/while/body/eval_jaxpr/psum | solution.py:30
  2164.4 79.1 %all-reduce.39.cloned.1.call-start = ((), (), s32[]{:S(2)}) async-start(), calls=%async_computation.7 | async-start | bytes 589824 | tf_op jit(solution)/shard_map/while/body/eval_jaxpr/psum | solution.py:67
  2302.1 79.1 %all-reduce.39.cloned.1.call-start = ((), (), s32[]{:S(2)}) async-start(), calls=%async_computation.7 | async-start | bytes 589824 | tf_op jit(solution)/shard_map/while/body/eval_jaxpr/psum | solution.py:67
  2439.7 79.1 %all-reduce.39.cloned.1.call-start = ((), (), s32[]{:S(2)}) async-start(), calls=%async_computation.7 | async-start | bytes 589824 | tf_op jit(solution)/shard_map/while/body/eval_jaxpr/psum | solution.py:67
  2485.4 70.5 %all-reduce.41.cloned.1.call-start = ((), (), s32[]{:S(2)}) async-start(), calls=%async_computation.8 | async-start | bytes 589824 | tf_op jit(solution)/shard_map/while/body/eval_jaxpr/psum | solution.py:30
  2587.8 79.7 %all-reduce.45.cloned.1.call-start = ((), (), s32[]{:S(2)}) async-start(), calls=%async_computation.10 | async-start | bytes 524288 | tf_op jit(solution)/shard_map/while/body/eval_jaxpr/psum | solution.py:67
  2633.4 70.6 %all-reduce.47.cloned.1.call-start = ((), (), s32[]{:S(2)}) async-start(), calls=%async_computation.11 | async-start | bytes 524288 | tf_op jit(solution)/shard_map/while/body/eval_jaxpr/psum | solution.py:30
  2724.8 78.8 %all-reduce.45.cloned.1.call-start = ((), (), s32[]{:S(2)}) async-start(), calls=%async_computation.10 | async-start | bytes 524288 | tf_op jit(solution)/shard_map/while/body/eval_jaxpr/psum | solution.py:67
  2860.9 78.8 %all-reduce.45.cloned.1.call-start = ((), (), s32[]{:S(2)}) async-start(), calls=%async_computation.10 | async-start | bytes 524288 | tf_op jit(solution)/shard_map/while/body/eval_jaxpr/psum | solution.py:67
  2996.9 78.8 %all-reduce.45.cloned.1.call-start = ((), (), s32[]{:S(2)}) async-start(), calls=%async_computation.10 | async-start | bytes 524288 | tf_op jit(solution)/shard_map/while/body/eval_jaxpr/psum | solution.py:67
  3132.8 79.7 %all-reduce.45.cloned.1.call-start = ((), (), s32[]{:S(2)}) async-start(), calls=%async_computation.10 | async-start | bytes 524288 | tf_op jit(solution)/shard_map/while/body/eval_jaxpr/psum | solution.py:67
  3178.4 70.6 %all-reduce.47.cloned.1.call-start = ((), (), s32[]{:S(2)}) async-start(), calls=%async_computation.11 | async-start | bytes 524288 | tf_op jit(solution)/shard_map/while/body/eval_jaxpr/psum | solution.py:30
  3269.8 78.8 %all-reduce.45.cloned.1.call-start = ((), (), s32[]{:S(2)}) async-start(), calls=%async_computation.10 | async-start | bytes 524288 | tf_op jit(solution)/shard_map/while/body/eval_jaxpr/psum | solution.py:67
  3411.0 78.5 %all-reduce.51.cloned.1.call-start = ((), (), s32[]{:S(2)}) async-start(), calls=%async_computation.13 | async-start | bytes 393216 | tf_op jit(solution)/shard_map/while/body/eval_jaxpr/psum | solution.py:67
  3541.0 78.5 %all-reduce.51.cloned.1.call-start = ((), (), s32[]{:S(2)}) async-start(), calls=%async_computation.13 | async-start | bytes 393216 | tf_op jit(solution)/shard_map/while/body/eval_jaxpr/psum | solution.py:67
  3671.1 79.4 %all-reduce.51.cloned.1.call-start = ((), (), s32[]{:S(2)}) async-start(), calls=%async_computation.13 | async-start | bytes 393216 | tf_op jit(solution)/shard_map/while/body/eval_jaxpr/psum | solution.py:67
  3802.0 78.5 %all-reduce.51.cloned.1.call-start = ((), (), s32[]{:S(2)}) async-start(), calls=%async_computation.13 | async-start | bytes 393216 | tf_op jit(solution)/shard_map/while/body/eval_jaxpr/psum | solution.py:67
  3931.9 78.5 %all-reduce.51.cloned.1.call-start = ((), (), s32[]{:S(2)}) async-start(), calls=%async_computation.13 | async-start | bytes 393216 | tf_op jit(solution)/shard_map/while/body/eval_jaxpr/psum | solution.py:67
  4061.8 78.5 %all-reduce.51.cloned.1.call-start = ((), (), s32[]{:S(2)}) async-start(), calls=%async_computation.13 | async-start | bytes 393216 | tf_op jit(solution)/shard_map/while/body/eval_jaxpr/psum | solution.py:67
  4197.0 79.1 %all-reduce.57.cloned.1.call-start = ((), (), s32[]{:S(2)}) async-start(), calls=%async_computation.16 | async-start | bytes 327680 | tf_op jit(solution)/shard_map/while/body/eval_jaxpr/psum | solution.py:67
  4330.8 78.3 %all-reduce.57.cloned.1.call-start = ((), (), s32[]{:S(2)}) async-start(), calls=%async_computation.16 | async-start | bytes 327680 | tf_op jit(solution)/shard_map/while/body/eval_jaxpr/psum | solution.py:67
  4463.8 78.3 %all-reduce.57.cloned.1.call-start = ((), (), s32[]{:S(2)}) async-start(), calls=%async_computation.16 | async-start | bytes 327680 | tf_op jit(solution)/shard_map/while/body/eval_jaxpr/psum | solution.py:67
  4596.8 78.3 %all-reduce.57.cloned.1.call-start = ((), (), s32[]{:S(2)}) async-start(), calls=%async_computation.16 | async-start | bytes 327680 | tf_op jit(solution)/shard_map/while/body/eval_jaxpr/psum | solution.py:67
  4729.8 79.1 %all-reduce.57.cloned.1.call-start = ((), (), s32[]{:S(2)}) async-start(), calls=%async_computation.16 | async-start | bytes 327680 | tf_op jit(solution)/shard_map/while/body/eval_jaxpr/psum | solution.py:67
  4863.5 78.3 %all-reduce.57.cloned.1.call-start = ((), (), s32[]{:S(2)}) async-start(), calls=%async_computation.16 | async-start | bytes 327680 | tf_op jit(solution)/shard_map/while/body/eval_jaxpr/psum | solution.py:67
  4998.9 77.9 %all-reduce.63.cloned.1.call-start = ((), (), s32[]{:S(2)}) async-start(), calls=%async_computation.19 | async-start | bytes 196608 | tf_op jit(solution)/shard_map/while/body/eval_jaxpr/psum | solution.py:67
  5127.7 77.9 %all-reduce.63.cloned.1.call-start = ((), (), s32[]{:S(2)}) async-start(), calls=%async_computation.19 | async-start | bytes 196608 | tf_op jit(solution)/shard_map/while/body/eval_jaxpr/psum | solution.py:67
  5256.4 78.7 %all-reduce.63.cloned.1.call-start = ((), (), s32[]{:S(2)}) async-start(), calls=%async_computation.19 | async-start | bytes 196608 | tf_op jit(solution)/shard_map/while/body/eval_jaxpr/psum | solution.py:67
  5385.8 77.9 %all-reduce.63.cloned.1.call-start = ((), (), s32[]{:S(2)}) async-start(), calls=%async_computation.19 | async-start | bytes 196608 | tf_op jit(solution)/shard_map/while/body/eval_jaxpr/psum | solution.py:67
  5514.6 77.9 %all-reduce.63.cloned.1.call-start = ((), (), s32[]{:S(2)}) async-start(), calls=%async_computation.19 | async-start | bytes 196608 | tf_op jit(solution)/shard_map/while/body/eval_jaxpr/psum | solution.py:67
  5643.3 77.9 %all-reduce.63.cloned.1.call-start = ((), (), s32[]{:S(2)}) async-start(), calls=%async_computation.19 | async-start | bytes 196608 | tf_op jit(solution)/shard_map/while/body/eval_jaxpr/psum | solution.py:67
  5773.1 78.5 %all-reduce.69.cloned.1.call-start = ((), (), s32[]{:S(2)}) async-start(), calls=%async_computation.22 | async-start | bytes 131072 | tf_op jit(solution)/shard_map/while/body/eval_jaxpr/psum | solution.py:67
  5902.3 77.7 %all-reduce.69.cloned.1.call-start = ((), (), s32[]{:S(2)}) async-start(), calls=%async_computation.22 | async-start | bytes 131072 | tf_op jit(solution)/shard_map/while/body/eval_jaxpr/psum | solution.py:67
  6030.5 77.6 %all-reduce.69.cloned.1.call-start = ((), (), s32[]{:S(2)}) async-start(), calls=%async_computation.22 | async-start | bytes 131072 | tf_op jit(solution)/shard_map/while/body/eval_jaxpr/psum | solution.py:67
  6158.6 77.6 %all-reduce.69.cloned.1.call-start = ((), (), s32[]{:S(2)}) async-start(), calls=%async_computation.22 | async-start | bytes 131072 | tf_op jit(solution)/shard_map/while/body/eval_jaxpr/psum | solution.py:67
  6286.9 78.5 %all-reduce.69.cloned.1.call-start = ((), (), s32[]{:S(2)}) async-start(), calls=%async_computation.22 | async-start | bytes 131072 | tf_op jit(solution)/shard_map/while/body/eval_jaxpr/psum | solution.py:67
  6415.8 77.7 %all-reduce.69.cloned.1.call-start = ((), (), s32[]{:S(2)}) async-start(), calls=%async_computation.22 | async-start | bytes 131072 | tf_op jit(solution)/shard_map/while/body/eval_jaxpr/psum | solution.py:67
  (80 other events, 4572.5 us)
Sparse Core Ops, SparseCore 0:
  110.9 35.6 all-reduce.28
  171.7 34.1 all-reduce.24
  253.5 35.6 all-reduce.28
  314.3 34.1 all-reduce.24
  360.1 34.5 all-reduce.26
  397.0 35.6 all-reduce.28
  457.9 34.1 all-reduce.24
  539.7 35.6 all-reduce.28
  600.5 34.1 all-reduce.24
  682.3 35.6 all-reduce.28
  743.1 34.1 all-reduce.24
  824.9 35.6 all-reduce.28
  893.0 34.1 all-reduce.30
  938.9 34.2 all-reduce.32
  975.6 35.3 all-reduce.34
  1034.7 34.0 all-reduce.30
  1116.1 35.3 all-reduce.34
  1175.2 34.0 all-reduce.30
  1256.6 35.3 all-reduce.34
  1315.7 34.0 all-reduce.30
  1397.1 35.3 all-reduce.34
  1456.2 34.0 all-reduce.30
  1502.0 34.2 all-reduce.32
  1538.5 35.3 all-reduce.34
  1597.6 34.0 all-reduce.30
  1679.0 35.3 all-reduce.34
  1750.7 34.0 all-reduce.36
  1831.8 34.5 all-reduce.40
  1888.2 34.1 all-reduce.36
  1969.6 34.5 all-reduce.40
  2026.1 34.1 all-reduce.36
  2071.7 34.1 all-reduce.38
  2108.1 34.5 all-reduce.40
  2164.5 34.1 all-reduce.36
  2245.7 34.5 all-reduce.40
  2302.2 34.1 all-reduce.36
  2383.4 34.5 all-reduce.40
  2439.8 34.1 all-reduce.36
  2521.1 34.6 all-reduce.40
  2587.9 34.1 all-reduce.42
  2669.9 34.0 all-reduce.46
  2724.9 34.1 all-reduce.42
  2806.0 34.0 all-reduce.46
  2861.0 34.1 all-reduce.42
  2941.9 34.0 all-reduce.46
  2997.0 34.1 all-reduce.42
  3077.9 34.0 all-reduce.46
  3132.9 34.1 all-reduce.42
  3214.8 34.0 all-reduce.46
  3269.9 34.1 all-reduce.42
  3350.8 34.0 all-reduce.46
  3411.1 34.1 all-reduce.48
  3541.1 34.1 all-reduce.48
  3671.2 34.1 all-reduce.48
  3802.1 34.1 all-reduce.48
  3932.0 34.1 all-reduce.48
  4061.9 34.1 all-reduce.48
  4197.1 34.1 all-reduce.54
  4330.9 34.0 all-reduce.54
  4464.0 34.0 all-reduce.54
  4596.9 34.0 all-reduce.54
  4729.9 34.0 all-reduce.54
  4863.7 34.0 all-reduce.54
  4999.0 34.0 all-reduce.60
  (80 shorter events, 2648.0 us)
where the time goes:
time: 6570 us; the launch traced here: 6550 us
  waiting for transfers between devices  4840 us (74%)
  other arithmetic  1330 us (20%)
  matrix products  233 us (4%)
  local copies, waits for them, and re-layouts  122 us (2%)
    psum x48, waiting for transfers between devices, transposed_panel(): return lax.psum(spread, 'row')  1640 us
    psum x48, waiting for transfers between devices, panel_step(): diag_fac = lax.psum(jnp.where(is_owner, diag_own, 0.0), 'row')  1610 us
    psum x48, waiting for transfers between devices, panel_step(): lax.psum(jnp.where(below_mask & own_col, solved_blocks, 0.0).astype(jnp.b...  1590 us
    another operation x144, other arithmetic, panel_step(): jnp.linalg.cholesky(jnp.where(is_owner, diag_blk, eye_blk))  596 us
    another operation x96, other arithmetic, panel_step(): lax.linalg.triangular_solve(diag_fac, col_blk, left_side=False, lower=Tru...  482 us
    dot_general x48, matrix products, panel_step(): lax.dot_general(row_panel.reshape(win_rows, blk_size), col_panel.reshape(...  209 us
  transfers between devices with their start and end apart: 144, of which 144 were waited for; matrix products, arithmetic and copies ran while one was open for 1% of the time, Pallas kernels for 0%

commit v1 on v0

v1 whole, which is shorter than its diff:
```python
import functools
import jax
import jax.numpy as jnp
from jax import lax
from jax.experimental import pallas as pl
from jax.experimental.pallas import tpu as pltpu
from jax.sharding import PartitionSpec as P

B = 128
NBLK = 48
G = 4
NLOC = 12
CH = 3
NCH = NLOC // CH
CR = CH * B
PANEL = 32
MESH = pl.DeviceIdType.MESH
NT = (((1,), (1,)), ((), ()))
TN = (((0,), (0,)), ((), ()))
F32 = jnp.float32
BF16 = jnp.bfloat16


def split3(x):
    hi = x.astype(BF16)
    rest = x - hi.astype(F32)
    mid = rest.astype(BF16)
    low = (rest - mid.astype(F32)).astype(BF16)
    return hi, mid, low


def left6(x, axis):
    hi, mid, low = split3(x)
    return jnp.concatenate([hi, mid, low, hi, mid, hi], axis=axis)


def right6(x, axis):
    hi, mid, low = split3(x)
    return jnp.concatenate([low, mid, hi, mid, hi, hi], axis=axis)


def dot(a, b, dims):
    return lax.dot_general(a, b, dims, preferred_element_type=F32)


def factor_panel(w, lane0):
    n = w.shape[0]
    cols = jnp.stack([jnp.broadcast_to(w[:, lane0 + j:lane0 + j + 1], (n, B)) for j in range(n)])
    sub = lax.broadcasted_iota(jnp.int32, (8, 2 * B), 0)
    groups = [w[8 * g:8 * g + 8] for g in range(n // 8)]
    for j in range(n):
        g0, s = j // 8, j % 8
        if s == 0 and j:
            cols = cols[:, 8:]
        inv = lax.rsqrt(cols[0, s:s + 1])
        fac = cols[0] * inv
        if j + 1 < n:
            cols = cols[1:] - fac[None] * fac[s + 1:, None, :]
        pivot = groups[g0][s:s + 1] * jnp.concatenate([inv, inv], axis=1)
        fac2 = jnp.concatenate([fac, fac], axis=1)
        head = groups[g0]
        groups[g0] = jnp.where(sub == s, pivot, jnp.where(sub > s, head - fac2[:8] * pivot, head))
        for g in range(g0 + 1, n // 8):
            groups[g] = groups[g] - fac2[8 * (g - g0):8 * (g - g0) + 8] * pivot
    return jnp.concatenate(groups, axis=0)


def factor_block(a):
    r = lax.broadcasted_iota(jnp.int32, (B, B), 0)
    c = lax.broadcasted_iota(jnp.int32, (B, B), 1)
    w = jnp.concatenate([a, jnp.where(r == c, 1.0, 0.0).astype(F32)], axis=1)
    done = []
    for p in range(B // PANEL):
        f = factor_panel(w[:PANEL], PANEL * p)
        done.append(f)
        if p + 1 < B // PANEL:
            w = w[PANEL:] - dot(left6(f[:, :B], 0), right6(f, 0), TN)[PANEL * (p + 1):]
    f = jnp.concatenate(done, axis=0)
    return f[:, :B], f[:, B:]


def kernel(a_ref, s_ref, rp, cp, cb, linv, ld, a_s, mcat, rhs_s, in_sem,
           inv_r, inv_s, cb_r, cb_s, rp_r, rp_s, cp_r, cp_s):
    bt = lax.axis_index("batch")
    r = lax.axis_index("row")
    c = lax.axis_index("col")

    def rows(i, n=B):
        return pl.ds(pl.multiple_of(i * B, B), n)

    def phase(k):
        return lax.div(k, 12)

    def base(k):
        p = phase(k)
        return 144 * p - 18 * p * (p - 1) + (k - 12 * p) * (12 - 3 * p)

    def chunk(k, q):
        return rows(base(k) + CH * (q - phase(k)), CR)

    def rcopy(buf, where, ssem, rsem, dev):
        return pltpu.make_async_remote_copy(
            src_ref=buf.at[where, :], dst_ref=buf.at[where, :], send_sem=ssem, recv_sem=rsem,
            device_id=dev, device_id_type=MESH)

    def inv_copy(k, j, dev):
        return rcopy(linv, rows(k), inv_s.at[k * 3 + j], inv_r.at[k], dev)

    def cb_copy(k, j, dev):
        return rcopy(cb, rows(k), cb_s.at[k * 4 + j], cb_r.at[k], dev)

    def rp_copy(k, q, j, dev):
        return rcopy(rp, chunk(k, q), rp_s.at[(k * 3 + j) * NCH + q], rp_r.at[k * NCH + q], dev)

    def cp_copy(k, q, j, dev):
        return rcopy(cp, chunk(k, q), cp_s.at[(k * 2 + j) * NCH + q], cp_r.at[k * NCH + q], dev)

    dest_a = jnp.where(lax.rem(c, 2) == 0, c + 1, c - 1)
    dest_b = jnp.where(c < 2, 2, 1)
    dest_e = jnp.where(c < 2, 3, 0)
    is_diag = r == c
    relays = (r == dest_b) & (r != c)

    def inv_send(k):
        return k < NBLK - 1

    load = pltpu.make_async_copy(a_ref, s_ref, in_sem)
    load.start()
    load.wait()

    def step(it, carry):
        k = it - 1
        kk = jnp.maximum(k, 0)
        kr = lax.rem(kk, G)
        nr = lax.rem(it, G)
        p = phase(kk)
        tk = lax.div(kk, G)
        tn = lax.div(it, G)

        @pl.when((k >= 0) & (c == kr))
        def _():
            @pl.when(r != kr)
            def _():
                inv_copy(kk, 0, (bt, kr, c)).wait_recv()

            mcat[...] = right6(linv[rows(kk), :], 1)

            @pl.when(r == nr)
            def _():
                x = dot(left6(s_ref[rows(tn), rows(tk)], 1), mcat[...], NT)
                cb[rows(kk), :] = x.astype(BF16)
                cb_copy(kk, 0, (bt, nr, nr)).start()

                @pl.when(k <= NBLK - 3)
                def _():
                    for j in range(1, G):
                        cb_copy(kk, j, (bt, lax.rem(nr + j, G), nr)).start()

            def solve(q, carry):
                x = s_ref[rows(CH * q, CR), rows(tk)]
                y = dot(left6(x, 1), mcat[...], NT)
                t = lax.broadcasted_iota(jnp.int32, (CR, B), 0) // B + CH * q
                below = t * G + r > kk
                s_ref[rows(CH * q, CR), rows(tk)] = jnp.where(below, y, x)
                rp[chunk(kk, q), :] = jnp.where(below, y, 0.0).astype(BF16)

                @pl.when(k <= NBLK - 3)
                def _():
                    for j in range(3):
                        rp_copy(kk, q, j, (bt, r, lax.rem(kr + 1 + j, G))).start()

                return carry

            lax.fori_loop(p, NCH, solve, 0)

        @pl.when((r == nr) & (c == nr))
        def _():
            a_s[...] = s_ref[rows(tn), rows(tn)]

            @pl.when(k >= 1)
            def _():
                kp = jnp.maximum(k - 1, 0)
                blk = rp[rows(base(kp) + tn - CH * phase(kp)), :]
                a_s[...] -= dot(blk, blk, NT)

            @pl.when(k >= 0)
            def _():
                cb_copy(kk, 0, (bt, r, kr)).wait_recv()
                blk = cb[rows(kk), :]
                a_s[...] -= dot(blk, blk, NT)

            u, m = factor_block(a_s[...])
            linv[rows(it), :] = m

            @pl.when(it < NBLK - 1)
            def _():
                for j in range(3):
                    inv_copy(it, j, (bt, lax.rem(nr + 1 + j, G), c)).start()

            low = jnp.transpose(u)
            i0 = lax.broadcasted_iota(jnp.int32, (B, B), 0)
            i1 = lax.broadcasted_iota(jnp.int32, (B, B), 1)
            ld[rows(tn), :] = jnp.where(i0 >= i1, low, 0.0)

        @pl.when((k >= 0) & (k <= NBLK - 3))
        def _():
            @pl.when((c == nr) & (r != nr))
            def _():
                cb_copy(kk, 0, (bt, nr, kr)).wait_recv()

            def take(q, carry):
                @pl.when(c != kr)
                def _():
                    rp_copy(kk, q, 0, (bt, r, kr)).wait_recv()

                @pl.when(is_diag & (k <= NBLK - 4))
                def _():
                    for j, d in ((0, dest_b), (1, dest_a)):
                        pltpu.make_async_remote_copy(
                            src_ref=rp.at[chunk(kk, q), :], dst_ref=cp.at[chunk(kk, q), :],
                            send_sem=cp_s.at[(kk * 2 + j) * NCH + q], recv_sem=cp_r.at[kk * NCH + q],
                            device_id=(bt, d, c), device_id_type=MESH).start()

                @pl.when(c == nr)
                def _():
                    s_ref[rows(CH * q, CR), rows(tn)] -= dot(rp[chunk(kk, q), :], cb[rows(kk), :], NT)

                return carry

            lax.fori_loop(p, NCH, take, 0)

        @pl.when((k >= 1) & (k <= NBLK - 3))
        def _():
            kp = jnp.maximum(k - 1, 0)
            pp = phase(kp)

            def arrive(q, carry):
                @pl.when(jnp.logical_not(is_diag))
                def _():
                    cp_copy(kp, q, 0, (bt, c, c)).wait_recv()

                @pl.when(relays)
                def _():
                    cp_copy(kp, q, 0, (bt, dest_e, c)).start()

                return carry

            lax.fori_loop(pp, NCH, arrive, 0)

            def by_col(cq, carry):
                @pl.when(is_diag)
                def _():
                    rhs_s[...] = rp[chunk(kp, cq), :]

                @pl.when(jnp.logical_not(is_diag))
                def _():
                    rhs_s[...] = cp[chunk(kp, cq), :]

                @pl.when((c == kr) & (lax.div(tk, CH) == cq))
                def _():
                    rhs_s[rows(lax.rem(tk, CH)), :] = jnp.zeros((B, B), BF16)

                def by_row(rq, carry):
                    s_ref[rows(CH * rq, CR), rows(CH * cq, CR)] -= dot(rp[chunk(kp, rq), :], rhs_s[...], NT)
                    return carry

                return lax.fori_loop(cq, NCH, by_row, carry)

            lax.fori_loop(pp, NCH, by_col, 0)

        return carry

    lax.fori_loop(0, NBLK, step, 0)

    def drain(k, carry):
        kr = lax.rem(k, G)
        nr = lax.rem(k + 1, G)
        p = phase(k)

        @pl.when((r == kr) & (c == kr) & (k < NBLK - 1))
        def _():
            for j in range(3):
                inv_copy(k, j, (bt, lax.rem(kr + 1 + j, G), c)).wait_send()

        @pl.when((r == nr) & (c == kr) & (k <= NBLK - 2))
        def _():
            cb_copy(k, 0, (bt, nr, nr)).wait_send()

            @pl.when(k <= NBLK - 3)
            def _():
                for j in range(1, G):
                    cb_copy(k, j, (bt, lax.rem(nr + j, G), nr)).wait_send()

        def each(q, carry):
            @pl.when((c == kr) & (k <= NBLK - 3))
            def _():
                for j in range(3):
                    rp_copy(k, q, j, (bt, r, lax.rem(kr + 1 + j, G))).wait_send()

            @pl.when(is_diag & (k <= NBLK - 4))
            def _():
                cp_copy(k, q, 0, (bt, dest_b, c)).wait_send()
                cp_copy(k, q, 1, (bt, dest_a, c)).wait_send()

            @pl.when(relays & (k <= NBLK - 4))
            def _():
                cp_copy(k, q, 0, (bt, dest_e, c)).wait_send()

            return carry

        return lax.fori_loop(p, NCH, each, carry)

    lax.fori_loop(0, NBLK, drain, 0)

    for t in range(NLOC):
        here = slice(t * B, (t + 1) * B)
        if t + 1 < NLOC:
            s_ref[here, (t + 1) * B:] = jnp.zeros((B, (NLOC - 1 - t) * B), F32)

        @pl.when(r < c)
        def _():
            s_ref[here, here] = jnp.zeros((B, B), F32)

        @pl.when(is_diag)
        def _():
            s_ref[here, here] = ld[here, :]


def solution(mesh):
    n = NLOC * B
    panels = (NCH * (NCH + 1) // 2) * 12 * CR

    def local(a_loc):
        dma = pltpu.SemaphoreType.DMA
        out = pl.pallas_call(
            kernel,
            out_shape=jax.ShapeDtypeStruct((n, n), F32),
            in_specs=[pl.BlockSpec(memory_space=pl.ANY)],
            out_specs=pl.BlockSpec(memory_space=pltpu.VMEM),
            scratch_shapes=[
                pltpu.VMEM((panels, B), BF16),
                pltpu.VMEM((panels, B), BF16),
                pltpu.VMEM((NBLK * B, B), BF16),
                pltpu.VMEM((NBLK * B, B), F32),
                pltpu.VMEM((n, B), F32),
                pltpu.VMEM((B, B), F32),
                pltpu.VMEM((B, 6 * B), BF16),
                pltpu.VMEM((CR, B), BF16),
                dma(()),
                dma((NBLK,)),
                dma((NBLK * 3,)),
                dma((NBLK,)),
                dma((NBLK * 4,)),
                dma((NBLK * NCH,)),
                dma((NBLK * 3 * NCH,)),
                dma((NBLK * NCH,)),
                dma((NBLK * 2 * NCH,)),
            ],
            compiler_params=pltpu.CompilerParams(has_side_effects=True, vmem_limit_bytes=62 << 20),
        )(a_loc.reshape(n, n))
        return out.reshape(a_loc.shape)

    spec = P(("batch", "row"), None, "col")
    return jax.shard_map(local, mesh=mesh, in_specs=(spec,), out_specs=spec, check_vma=False)
```

time: 6570 us -> 554 us (0.08)
  waiting for transfers between devices: 4840 us -> 0 us
  other arithmetic: 1330 us -> 0 us
  Pallas kernels: 0 us -> 545 us
  matrix products: 233 us -> 0 us
  local copies, waits for them, and re-layouts: 122 us -> 8.27 us
    psum x144 -> x0, waiting for transfers between devices: 4830 us -> none  [the longest x48 1640 us: transposed_panel(): return lax.psum(spread, 'row')]
    another operation x240 -> x0, other arithmetic: 1080 us -> none  [the longest x144 596 us: panel_step(): jnp.linalg.cholesky(jnp.where(is_owner, diag_blk, eye_blk))]
    pallas_call x0 -> x1, Pallas kernels: none -> 545 us  [local(): pl.pallas_call(kernel, out_shape=jax.ShapeDtypeStruct((n, n), F32), in_sp...]
    dot_general x48 -> x0, matrix products: 209 us -> none  [panel_step(): lax.dot_general(row_panel.reshape(win_rows, blk_size), col_panel.reshape(...]
    select_n x97 -> x0, other arithmetic: 99.5 us -> none  [the longest x48 59.1 us: panel_step(): diag_fac = lax.psum(jnp.where(is_owner, diag_own, 0.0), 'row')]
    mul x48 -> x0, other arithmetic: 78.5 us -> none  [transposed_panel(): row_panel[:, None] * pick_mask.astype(jnp.bfloat16)[None, :, None, None]]
  transfers between devices with their start and end apart: 144 -> 0, of which waited for: 144 -> 0; matrix products, arithmetic and copies ran while one was open for 1% -> 0% of each run, Pallas kernels for 0% -> 0%
where the time goes in v1:
time: 554 us
  Pallas kernels  545 us (98%)
  local copies, waits for them, and re-layouts  8.27 us (1%)
    pallas_call x1, Pallas kernels, local(): pl.pallas_call(kernel, out_shape=jax.ShapeDtypeStruct((n, n), F32), in_sp...  545 us

profile of v1, /device:TPU:31, one launch (start us, length us, event | category | flops | bytes accessed | tf_op | source)
XLA Modules:
  0.0 553.7 jit_solution(7957662594666192455)
XLA Ops:
  0.0 545.4 %shard_map.17 = f32[1536,1536]{1,0:T(8,128)} custom-call(f32[1536,1536]{1,0:T(8,128)} %bitcast.3), custom_call_target="tpu_custom_call" | custom-call | tf_op jit(solution)/shard_map/pallas_call | solution.py:335
  545.4 8.3 %copy.3 = f32[12,128,1536]{2,1,0:T(8,128)} copy(f32[12,128,1536]{2,1,0:T(8,128)} %bitcast.2) | data formatting | bytes 18874368

commit v2 on v1

--- a/solution.py
+++ b/solution.py
@@ -48,21 +48,28 @@
     cols = jnp.stack([jnp.broadcast_to(w[:, lane0 + j:lane0 + j + 1], (n, B)) for j in range(n)])
     sub = lax.broadcasted_iota(jnp.int32, (8, 2 * B), 0)
     groups = [w[8 * g:8 * g + 8] for g in range(n // 8)]
+    scales = [jnp.zeros((8, 2 * B), F32) for g in range(n // 8)]
+
+    def twice(v):
+        return jnp.concatenate([v, v], axis=1)
+
     for j in range(n):
         g0, s = j // 8, j % 8
         if s == 0 and j:
             cols = cols[:, 8:]
-        inv = lax.rsqrt(cols[0, s:s + 1])
-        fac = cols[0] * inv
+        col = cols[0]
+        pivot = col[s:s + 1]
+        fac = col * (1.0 / pivot)
         if j + 1 < n:
-            cols = cols[1:] - fac[None] * fac[s + 1:, None, :]
-        pivot = groups[g0][s:s + 1] * jnp.concatenate([inv, inv], axis=1)
-        fac2 = jnp.concatenate([fac, fac], axis=1)
-        head = groups[g0]
-        groups[g0] = jnp.where(sub == s, pivot, jnp.where(sub > s, head - fac2[:8] * pivot, head))
+            cols = cols[1:] - fac[None] * col[s + 1:, None, :]
+        fac2 = twice(fac)
+        row = groups[g0][s:s + 1]
+        scales[g0] = jnp.where(sub == s, twice(lax.rsqrt(pivot)), scales[g0])
+        if s < 7:
+            groups[g0] = groups[g0] - jnp.where(sub > s, fac2[:8], 0.0) * row
         for g in range(g0 + 1, n // 8):
-            groups[g] = groups[g] - fac2[8 * (g - g0):8 * (g - g0) + 8] * pivot
-    return jnp.concatenate(groups, axis=0)
+            groups[g] = groups[g] - fac2[8 * (g - g0):8 * (g - g0) + 8] * row
+    return jnp.concatenate([g * f for g, f in zip(groups, scales)], axis=0)
 
 
 def factor_block(a):
@@ -79,7 +86,11 @@
     return f[:, :B], f[:, B:]
 
 
-def kernel(a_ref, s_ref, rp, cp, cb, linv, ld, a_s, mcat, rhs_s, in_sem,
+SPREAD = ((0, 1, 1, 0), (0, 2, 2, 0), (0, 3, 3, 0), (1, 0, 2, 1), (1, 0, 0, 1), (1, 0, 3, 1),
+          (2, 3, 1, 2), (2, 3, 3, 2), (2, 3, 0, 2), (3, 2, 2, 3), (3, 1, 1, 3), (3, 0, 0, 3))
+
+
+def kernel(a_ref, s_ref, rp, cp, cb, linv, ld, a_s, mcat, rhs_s, last_s, in_sem,
            inv_r, inv_s, cb_r, cb_s, rp_r, rp_s, cp_r, cp_s):
     bt = lax.axis_index("batch")
     r = lax.axis_index("row")
@@ -113,16 +124,31 @@
         return rcopy(rp, chunk(k, q), rp_s.at[(k * 3 + j) * NCH + q], rp_r.at[k * NCH + q], dev)
 
     def cp_copy(k, q, j, dev):
-        return rcopy(cp, chunk(k, q), cp_s.at[(k * 2 + j) * NCH + q], cp_r.at[k * NCH + q], dev)
-
-    dest_a = jnp.where(lax.rem(c, 2) == 0, c + 1, c - 1)
-    dest_b = jnp.where(c < 2, 2, 1)
-    dest_e = jnp.where(c < 2, 3, 0)
+        return pltpu.make_async_remote_copy(
+            src_ref=rp.at[chunk(k, q), :], dst_ref=cp.at[chunk(k, q), :],
+            send_sem=cp_s.at[(k * 3 + j) * NCH + q], recv_sem=cp_r.at[k * NCH + q],
+            device_id=dev, device_id_type=MESH)
+
+    def spread(k, q, act):
+        count = {}
+        for sr, sc, dr, dc in SPREAD:
+            j = count.get((sr, sc), 0)
+            count[(sr, sc)] = j + 1
+
+            @pl.when((r == sr) & (c == sc))
+            def _():
+                act(cp_copy(k, q, j, (bt, dr, dc)))
+
     is_diag = r == c
-    relays = (r == dest_b) & (r != c)
-
-    def inv_send(k):
-        return k < NBLK - 1
+
+    def row_target(kr, j):
+        twin = kr + 1 - 2 * lax.rem(kr, 2)
+        entry = 2 - 2 * lax.div(kr, 2)
+        first_twin = lax.rem(kr, 2) == 0
+        return jnp.where(first_twin, twin, entry) if j == 0 else jnp.where(first_twin, entry, twin)
+
+    def passes_on(kr):
+        return c == 2 - 2 * lax.div(kr, 2)
 
     load = pltpu.make_async_copy(a_ref, s_ref, in_sem)
     load.start()
@@ -166,8 +192,8 @@
 
                 @pl.when(k <= NBLK - 3)
                 def _():
-                    for j in range(3):
-                        rp_copy(kk, q, j, (bt, r, lax.rem(kr + 1 + j, G))).start()
+                    for j in range(2):
+                        rp_copy(kk, q, j, (bt, r, row_target(kr, j))).start()
 
                 return carry
 
@@ -177,11 +203,12 @@
         def _():
             a_s[...] = s_ref[rows(tn), rows(tn)]
 
-            @pl.when(k >= 1)
-            def _():
-                kp = jnp.maximum(k - 1, 0)
-                blk = rp[rows(base(kp) + tn - CH * phase(kp)), :]
-                a_s[...] -= dot(blk, blk, NT)
+            for back in (2, 1):
+                @pl.when(k >= back)
+                def _():
+                    kp = jnp.maximum(k - back, 0)
+                    blk = rp[rows(base(kp) + tn - CH * phase(kp)), :]
+                    a_s[...] -= dot(blk, blk, NT)
 
             @pl.when(k >= 0)
             def _():
@@ -208,18 +235,38 @@
             def _():
                 cb_copy(kk, 0, (bt, nr, kr)).wait_recv()
 
+            k1 = jnp.maximum(k - 1, 0)
+            qn = lax.div(tn, CH)
+
+            @pl.when((c == nr) & (k >= 1))
+            def _():
+                @pl.when(is_diag)
+                def _():
+                    last_s[...] = rp[rows(base(k1) + tn - CH * phase(k1)), :]
+
+                @pl.when(jnp.logical_not(is_diag))
+                def _():
+                    cp_copy(k1, qn, 0, (bt, r, c)).wait_recv()
+                    last_s[...] = cp[rows(base(k1) + tn - CH * phase(k1)), :]
+
+                def catch_up(q, carry):
+                    s_ref[rows(CH * q, CR), rows(tn)] -= dot(rp[chunk(k1, q), :], last_s[...], NT)
+                    return carry
+
+                lax.fori_loop(p, NCH, catch_up, 0)
+
             def take(q, carry):
                 @pl.when(c != kr)
                 def _():
                     rp_copy(kk, q, 0, (bt, r, kr)).wait_recv()
 
-                @pl.when(is_diag & (k <= NBLK - 4))
-                def _():
-                    for j, d in ((0, dest_b), (1, dest_a)):
-                        pltpu.make_async_remote_copy(
-                            src_ref=rp.at[chunk(kk, q), :], dst_ref=cp.at[chunk(kk, q), :],
-                            send_sem=cp_s.at[(kk * 2 + j) * NCH + q], recv_sem=cp_r.at[kk * NCH + q],
-                            device_id=(bt, d, c), device_id_type=MESH).start()
+                @pl.when(passes_on(kr))
+                def _():
+                    rp_copy(kk, q, 2, (bt, r, c + 1)).start()
+
+                @pl.when(k <= NBLK - 4)
+                def _():
+                    spread(kk, q, lambda copy: copy.start())
 
                 @pl.when(c == nr)
                 def _():
@@ -229,23 +276,12 @@
 
             lax.fori_loop(p, NCH, take, 0)
 
-        @pl.when((k >= 1) & (k <= NBLK - 3))
-        def _():
-            kp = jnp.maximum(k - 1, 0)
+        @pl.when(k >= 2)
+        def _():
+            kp = jnp.maximum(k - 2, 0)
+            k1 = jnp.maximum(k - 1, 0)
             pp = phase(kp)
-
-            def arrive(q, carry):
-                @pl.when(jnp.logical_not(is_diag))
-                def _():
-                    cp_copy(kp, q, 0, (bt, c, c)).wait_recv()
-
-                @pl.when(relays)
-                def _():
-                    cp_copy(kp, q, 0, (bt, dest_e, c)).start()
-
-                return carry
-
-            lax.fori_loop(pp, NCH, arrive, 0)
+            t1 = lax.div(k1, G)
 
             def by_col(cq, carry):
                 @pl.when(is_diag)
@@ -254,11 +290,19 @@
 
                 @pl.when(jnp.logical_not(is_diag))
                 def _():
+                    @pl.when(jnp.logical_not((c == kr) & (lax.div(tk, CH) == cq)))
+                    def _():
+                        cp_copy(kp, cq, 0, (bt, r, c)).wait_recv()
+
                     rhs_s[...] = cp[chunk(kp, cq), :]
 
                 @pl.when((c == kr) & (lax.div(tk, CH) == cq))
                 def _():
                     rhs_s[rows(lax.rem(tk, CH)), :] = jnp.zeros((B, B), BF16)
+
+                @pl.when((c == lax.rem(k1, G)) & (lax.div(t1, CH) == cq))
+                def _():
+                    rhs_s[rows(lax.rem(t1, CH)), :] = jnp.zeros((B, B), BF16)
 
                 def by_row(rq, carry):
                     s_ref[rows(CH * rq, CR), rows(CH * cq, CR)] -= dot(rp[chunk(kp, rq), :], rhs_s[...], NT)
@@ -294,17 +338,16 @@
         def each(q, carry):
             @pl.when((c == kr) & (k <= NBLK - 3))
             def _():
-                for j in range(3):
-                    rp_copy(k, q, j, (bt, r, lax.rem(kr + 1 + j, G))).wait_send()
-
-            @pl.when(is_diag & (k <= NBLK - 4))
-            def _():
-                cp_copy(k, q, 0, (bt, dest_b, c)).wait_send()
-                cp_copy(k, q, 1, (bt, dest_a, c)).wait_send()
-
-            @pl.when(relays & (k <= NBLK - 4))
-            def _():
-                cp_copy(k, q, 0, (bt, dest_e, c)).wait_send()
+                for j in range(2):
+                    rp_copy(k, q, j, (bt, r, row_target(kr, j))).wait_send()
+
+            @pl.when(passes_on(kr) & (k <= NBLK - 3))
+            def _():
+                rp_copy(k, q, 2, (bt, r, c + 1)).wait_send()
+
+            @pl.when(k <= NBLK - 4)
+            def _():
+                spread(k, q, lambda copy: copy.wait_send())
 
             return carry
 
@@ -346,6 +389,7 @@
                 pltpu.VMEM((B, B), F32),
                 pltpu.VMEM((B, 6 * B), BF16),
                 pltpu.VMEM((CR, B), BF16),
+                pltpu.VMEM((B, B), BF16),
                 dma(()),
                 dma((NBLK,)),
                 dma((NBLK * 3,)),
@@ -354,7 +398,7 @@
                 dma((NBLK * NCH,)),
                 dma((NBLK * 3 * NCH,)),
                 dma((NBLK * NCH,)),
-                dma((NBLK * 2 * NCH,)),
+                dma((NBLK * 3 * NCH,)),
             ],
             compiler_params=pltpu.CompilerParams(has_side_effects=True, vmem_limit_bytes=62 << 20),
         )(a_loc.reshape(n, n))

time: 554 us -> 531 us (0.958)
  Pallas kernels: 545 us -> 523 us
    pallas_call x1, Pallas kernels: 545 us -> 523 us  [local(): pl.pallas_call(kernel, out_shape=jax.ShapeDtypeStruct((n, n), F32), in_sp...]
where the time goes in v2:
time: 531 us
  Pallas kernels  523 us (98%)
  local copies, waits for them, and re-layouts  8.27 us (2%)
    pallas_call x1, Pallas kernels, local(): pl.pallas_call(kernel, out_shape=jax.ShapeDtypeStruct((n, n), F32), in_sp...  523 us

profile of v2, /device:TPU:31, one launch (start us, length us, event | category | flops | bytes accessed | tf_op | source)
XLA Modules:
  0.0 531.0 jit_solution(8817026960813796719)
XLA Ops:
  0.0 522.7 %shard_map.17 = f32[1536,1536]{1,0:T(8,128)} custom-call(f32[1536,1536]{1,0:T(8,128)} %bitcast.3), custom_call_target="tpu_custom_call" | custom-call | tf_op jit(solution)/shard_map/pallas_call | solution.py:378
  522.7 8.3 %copy.3 = f32[12,128,1536]{2,1,0:T(8,128)} copy(f32[12,128,1536]{2,1,0:T(8,128)} %bitcast.2) | data formatting | bytes 18874368

commit v3 on v2

--- a/solution.py
+++ b/solution.py
@@ -90,7 +90,7 @@
           (2, 3, 1, 2), (2, 3, 3, 2), (2, 3, 0, 2), (3, 2, 2, 3), (3, 1, 1, 3), (3, 0, 0, 3))
 
 
-def kernel(a_ref, s_ref, rp, cp, cb, linv, ld, a_s, mcat, rhs_s, last_s, in_sem,
+def kernel(a_ref, s_ref, rp, cp, cb, linv, ld, a_s, mcat, rhs_s, last_s, in_sem, first_sem,
            inv_r, inv_s, cb_r, cb_s, rp_r, rp_s, cp_r, cp_s):
     bt = lax.axis_index("batch")
     r = lax.axis_index("row")
@@ -150,9 +150,11 @@
     def passes_on(kr):
         return c == 2 - 2 * lax.div(kr, 2)
 
+    first = pltpu.make_async_copy(a_ref.at[0:B, 0:B], a_s, first_sem)
+    first.start()
     load = pltpu.make_async_copy(a_ref, s_ref, in_sem)
     load.start()
-    load.wait()
+    first.wait()
 
     def step(it, carry):
         k = it - 1
@@ -201,7 +203,9 @@
 
         @pl.when((r == nr) & (c == nr))
         def _():
-            a_s[...] = s_ref[rows(tn), rows(tn)]
+            @pl.when(it > 0)
+            def _():
+                a_s[...] = s_ref[rows(tn), rows(tn)]
 
             for back in (2, 1):
                 @pl.when(k >= back)
@@ -229,52 +233,9 @@
             i1 = lax.broadcasted_iota(jnp.int32, (B, B), 1)
             ld[rows(tn), :] = jnp.where(i0 >= i1, low, 0.0)
 
-        @pl.when((k >= 0) & (k <= NBLK - 3))
-        def _():
-            @pl.when((c == nr) & (r != nr))
-            def _():
-                cb_copy(kk, 0, (bt, nr, kr)).wait_recv()
-
-            k1 = jnp.maximum(k - 1, 0)
-            qn = lax.div(tn, CH)
-
-            @pl.when((c == nr) & (k >= 1))
-            def _():
-                @pl.when(is_diag)
-                def _():
-                    last_s[...] = rp[rows(base(k1) + tn - CH * phase(k1)), :]
-
-                @pl.when(jnp.logical_not(is_diag))
-                def _():
-                    cp_copy(k1, qn, 0, (bt, r, c)).wait_recv()
-                    last_s[...] = cp[rows(base(k1) + tn - CH * phase(k1)), :]
-
-                def catch_up(q, carry):
-                    s_ref[rows(CH * q, CR), rows(tn)] -= dot(rp[chunk(k1, q), :], last_s[...], NT)
-                    return carry
-
-                lax.fori_loop(p, NCH, catch_up, 0)
-
-            def take(q, carry):
-                @pl.when(c != kr)
-                def _():
-                    rp_copy(kk, q, 0, (bt, r, kr)).wait_recv()
-
-                @pl.when(passes_on(kr))
-                def _():
-                    rp_copy(kk, q, 2, (bt, r, c + 1)).start()
-
-                @pl.when(k <= NBLK - 4)
-                def _():
-                    spread(kk, q, lambda copy: copy.start())
-
-                @pl.when(c == nr)
-                def _():
-                    s_ref[rows(CH * q, CR), rows(tn)] -= dot(rp[chunk(kk, q), :], cb[rows(kk), :], NT)
-
-                return carry
-
-            lax.fori_loop(p, NCH, take, 0)
+        @pl.when(it == 0)
+        def _():
+            load.wait()
 
         @pl.when(k >= 2)
         def _():
@@ -311,6 +272,53 @@
                 return lax.fori_loop(cq, NCH, by_row, carry)
 
             lax.fori_loop(pp, NCH, by_col, 0)
+
+        @pl.when((k >= 0) & (k <= NBLK - 3))
+        def _():
+            @pl.when((c == nr) & (r != nr))
+            def _():
+                cb_copy(kk, 0, (bt, nr, kr)).wait_recv()
+
+            k1 = jnp.maximum(k - 1, 0)
+            qn = lax.div(tn, CH)
+
+            @pl.when((c == nr) & (k >= 1))
+            def _():
+                @pl.when(is_diag)
+                def _():
+                    last_s[...] = rp[rows(base(k1) + tn - CH * phase(k1)), :]
+
+                @pl.when(jnp.logical_not(is_diag))
+                def _():
+                    cp_copy(k1, qn, 0, (bt, r, c)).wait_recv()
+                    last_s[...] = cp[rows(base(k1) + tn - CH * phase(k1)), :]
+
+                def catch_up(q, carry):
+                    s_ref[rows(CH * q, CR), rows(tn)] -= dot(rp[chunk(k1, q), :], last_s[...], NT)
+                    return carry
+
+                lax.fori_loop(p, NCH, catch_up, 0)
+
+            def take(q, carry):
+                @pl.when(c != kr)
+                def _():
+                    rp_copy(kk, q, 0, (bt, r, kr)).wait_recv()
+
+                @pl.when(passes_on(kr))
+                def _():
+                    rp_copy(kk, q, 2, (bt, r, c + 1)).start()
+
+                @pl.when(c == nr)
+                def _():
+                    s_ref[rows(CH * q, CR), rows(tn)] -= dot(rp[chunk(kk, q), :], cb[rows(kk), :], NT)
+
+                @pl.when(k <= NBLK - 4)
+                def _():
+                    spread(kk, q, lambda copy: copy.start())
+
+                return carry
+
+            lax.fori_loop(p, NCH, take, 0)
 
         return carry
 
@@ -391,6 +399,7 @@
                 pltpu.VMEM((CR, B), BF16),
                 pltpu.VMEM((B, B), BF16),
                 dma(()),
+                dma(()),
                 dma((NBLK,)),
                 dma((NBLK * 3,)),
                 dma((NBLK,)),

time: 531 us -> 515 us (0.970)
  Pallas kernels: 523 us -> 506 us
    pallas_call x1, Pallas kernels: 523 us -> 506 us  [local(): pl.pallas_call(kernel, out_shape=jax.ShapeDtypeStruct((n, n), F32), in_sp...]
where the time goes in v3:
time: 515 us
  Pallas kernels  506 us (98%)
  local copies, waits for them, and re-layouts  8.27 us (2%)
    pallas_call x1, Pallas kernels, local(): pl.pallas_call(kernel, out_shape=jax.ShapeDtypeStruct((n, n), F32), in_sp...  506 us

profile of v3, /device:TPU:31, one launch (start us, length us, event | category | flops | bytes accessed | tf_op | source)
XLA Modules:
  0.0 514.6 jit_solution(16585994126177623960)
XLA Ops:
  0.0 506.3 %shard_map.17 = f32[1536,1536]{1,0:T(8,128)} custom-call(f32[1536,1536]{1,0:T(8,128)} %bitcast.3), custom_call_target="tpu_custom_call" | custom-call | tf_op jit(solution)/shard_map/pallas_call | solution.py:386
  506.3 8.3 %copy.3 = f32[12,128,1536]{2,1,0:T(8,128)} copy(f32[12,128,1536]{2,1,0:T(8,128)} %bitcast.2) | data formatting | bytes 18874368
